TPU v7x, 32 devices: a whole 2x2x4 slice. The times are simulated.
32 devices in a mesh: expert: 4 (over x, core), shard: 8 (over z, y).
Axes of the slice: x: 2, y: 2, z: 4, core: 2. Of those that a mesh axis runs over, the one named last changes fastest.
Arguments:
- master_gate: float32 [128, 2048, 768], P('expert', 'shard'), may hold values from -0.125 to 0.125
- master_up: float32 [128, 2048, 768], P('expert', 'shard'), may hold values from -0.125 to 0.125
- router_weight: float32 [2048, 128], P('shard', 'expert'), may hold values from -0.125 to 0.125
- router_gain: float32 [2048], P('shard'), may hold values from 0.25 to 1.75
Outputs:
- final_gate: bfloat16 [128, 768, 2048], P('expert', 'shard')
- final_up: bfloat16 [128, 768, 2048], P('expert', 'shard')
- serve_router: bfloat16 [2048, 128], replicated
All inputs are finite; a program needn't handle non-finite values.
Results may differ from a plain program's by a relative error of at most 0.001.
Values may be sent and summed in bfloat16 or wider, within the bound.
A program may use at most 192 MiB of HBM per device.

v0:
```python
import functools

import jax
import jax.numpy as jnp
from jax import lax
from jax.experimental import pallas as pl
from jax.experimental.pallas import tpu as pltpu
from jax.sharding import PartitionSpec as P

NEAR = 1
PAIR = 2
CHUNK = 2
SLOTS = 4
LIMIT = 32


def plain(master_gate, master_up, router_weight, router_gain):
    narrow_gate, narrow_up = (master_gate.astype(jnp.bfloat16), master_up.astype(jnp.bfloat16))
    final_gate, final_up = (
        lax.all_to_all(narrow_gate, "shard", split_axis=2, concat_axis=1, tiled=True),
        lax.all_to_all(narrow_up, "shard", split_axis=2, concat_axis=1, tiled=True),
    )
    final_gate = jnp.transpose(final_gate, (0, 2, 1))
    final_up = jnp.transpose(final_up, (0, 2, 1))
    part_router = (router_weight * router_gain[:, None]).astype(jnp.bfloat16)
    row_router = lax.all_gather(part_router, "shard", axis=0, tiled=True)
    serve_router = lax.all_gather(row_router, "expert", axis=1, tiled=True)
    return (final_gate, final_up, serve_router)


def kernel(
    shards, groups, gate, up, weight, gain, out_gate, out_up, out_router,
    held, coming, router, load_sem, own_sem, send_sem, recv_sem,
    row_send, row_recv, column_send, column_recv,
):
    me, group = lax.axis_index("shard"), lax.axis_index("expert")
    _, _, experts, rows, depth = held.shape
    width = weight.shape[0]
    chunks = experts // CHUNK
    sources, outs = (gate, up), (out_gate, out_up)
    mine = pl.ds(pl.multiple_of(me * depth, depth), depth)
    my_part = pl.ds(pl.multiple_of(group * width, width), width)

    barrier = pltpu.get_barrier_semaphore()
    for step in range(1, shards):
        pl.semaphore_signal(barrier, inc=1, device_id={"shard": lax.rem(me + step, shards)})
    for step in range(1, groups):
        pl.semaphore_signal(barrier, inc=1, device_id={"expert": lax.rem(group + step, groups)})

    def load(which, expert):
        slot = lax.rem(expert, SLOTS)
        return pltpu.make_async_copy(sources[which].at[expert], coming.at[slot], load_sem.at[slot])

    def own(which, span):
        return pltpu.make_async_copy(
            held.at[which, me, span], outs[which].at[span, :, mine], own_sem.at[which]
        )

    def send(which, peer, span):
        return pltpu.make_async_remote_copy(
            src_ref=held.at[which, peer, span],
            dst_ref=outs[which].at[span, :, mine],
            send_sem=send_sem.at[which, peer],
            recv_sem=recv_sem.at[which, me],
            device_id={"shard": peer},
        )

    def arrival(which, peer):
        there = pl.ds(pl.multiple_of(peer * depth, depth), depth)
        return pltpu.make_async_remote_copy(
            src_ref=held.at[which, peer],
            dst_ref=outs[which].at[:, :, there],
            send_sem=send_sem.at[which, peer],
            recv_sem=recv_sem.at[which, peer],
            device_id={"shard": peer},
        )

    def row(peer):
        return pltpu.make_async_remote_copy(
            src_ref=router.at[me, my_part],
            dst_ref=router.at[me, my_part],
            send_sem=row_send.at[peer],
            recv_sem=row_recv.at[me],
            device_id={"shard": peer},
        )

    def row_arrival(peer):
        return pltpu.make_async_remote_copy(
            src_ref=router.at[peer, my_part],
            dst_ref=router.at[peer, my_part],
            send_sem=row_send.at[peer],
            recv_sem=row_recv.at[peer],
            device_id={"shard": peer},
        )

    def column(peer, of):
        part = pl.ds(pl.multiple_of(of * width, width), width)
        return pltpu.make_async_remote_copy(
            src_ref=router.at[:, part],
            dst_ref=router.at[:, part],
            send_sem=column_send.at[peer],
            recv_sem=column_recv.at[of],
            device_id={"expert": peer},
        )

    def to_peers(least, most, act):
        place, side = me // PAIR, lax.rem(me, PAIR)
        for away in range(least, most + 1):
            for turned in range(0 if away else 1, PAIR):
                other = lax.rem(side + turned, PAIR)
                if away == 0:
                    act(place * PAIR + other)
                    continue

                @pl.when(place + away < shards // PAIR)
                def _():
                    act((place + away) * PAIR + other)

                @pl.when(place >= away)
                def _():
                    act((place - away) * PAIR + other)

    last = shards // PAIR - 1
    for first in range(SLOTS):
        load(0, first).start()
    router[me, my_part] = (weight[...] * gain[...]).astype(jnp.bfloat16)

    def turn(which, expert):
        load(which, expert).wait()
        block = coming[lax.rem(expert, SLOTS)].T.astype(jnp.bfloat16)
        for peer in range(shards):
            held[which, peer, expert] = block[peer * rows:(peer + 1) * rows]

        @pl.when(expert + SLOTS < experts)
        def _():
            load(which, expert + SLOTS).start()

    def turns(which, chunk):
        @pl.loop(0, CHUNK)
        def _(step):
            turn(which, chunk * CHUNK + step)

    def near(which, chunk):
        span = pl.ds(chunk * CHUNK, CHUNK)
        to_peers(0, NEAR, lambda peer: send(which, peer, span).start())
        own(which, span).start()

    for which in range(2):
        turns(which, 0)
        if which == 0:
            pl.semaphore_wait(barrier, shards + groups - 2)
            to_peers(0, last, lambda peer: row(peer).start())
        else:
            near(0, chunks - 1)

        @pl.loop(1, chunks)
        def _(chunk):
            turns(which, chunk)
            near(which, chunk - 1)

        if which == 0:
            for first in range(SLOTS):
                load(1, first).start()
    near(1, chunks - 1)
    whole = pl.ds(0, experts)
    for away in range(NEAR + 1, last + 1):
        for which in range(2):
            to_peers(away, away, lambda peer: send(which, peer, whole).start())

    to_peers(0, last, lambda peer: row_arrival(peer).wait_recv())
    for step in range(1, groups):
        column(lax.rem(group + step, groups), group).start()
    for step in range(1, groups):
        peer = lax.rem(group + step, groups)
        column(peer, peer).wait_recv()
    for shard in range(shards):
        out_router[shard * depth:(shard + 1) * depth] = router[shard].T
    to_peers(0, last, lambda peer: row(peer).wait_send())
    for step in range(1, groups):
        column(lax.rem(group + step, groups), group).wait_send()

    for which in range(2):
        own(which, whole).wait()
        to_peers(0, last, lambda peer: arrival(which, peer).wait())


def put_out(gate, up, router, out_gate, out_up, out_router, sem):
    copies = [
        pltpu.make_async_copy(source, out, sem.at[at])
        for at, (source, out) in enumerate(((gate, out_gate), (up, out_up), (router, out_router)))
    ]
    for copy in copies:
        copy.start()
    for copy in copies:
        copy.wait()


def per_device(shards, groups, master_gate, master_up, router_weight, router_gain):
    experts, depth, inner = master_gate.shape
    width = router_weight.shape[1]
    rows = inner // shards
    if shards % PAIR or depth % 128 or rows % 16 or width % 16 or experts % CHUNK or experts < 2 * CHUNK or (width * groups) % 128:
        return plain(master_gate, master_up, router_weight, router_gain)
    anywhere = pl.BlockSpec(memory_space=pl.ANY)
    inside = pl.BlockSpec(memory_space=pltpu.VMEM)
    final = pltpu.VMEM((experts, rows, shards * depth), jnp.bfloat16)
    dma = pltpu.SemaphoreType.DMA
    kept = pl.pallas_call(
        functools.partial(kernel, shards, groups),
        out_shape=(final, final, pltpu.VMEM((shards * depth, groups * width), jnp.bfloat16)),
        in_specs=[anywhere, anywhere, inside, inside],
        out_specs=(inside, inside, inside),
        scratch_shapes=[
            pltpu.VMEM((2, shards, experts, rows, depth), jnp.bfloat16),
            pltpu.VMEM((SLOTS, depth, inner), jnp.float32),
            pltpu.VMEM((shards, groups * width, depth), jnp.bfloat16),
            dma((SLOTS,)), dma((2,)), dma((2, shards)), dma((2, shards)),
            dma((shards,)), dma((shards,)), dma((groups,)), dma((groups,)),
        ],
        compiler_params=pltpu.CompilerParams(
            collective_id=0, has_side_effects=True, vmem_limit_bytes=LIMIT * 2**20
        ),
    )(master_gate, master_up, router_weight.T, router_gain[None])
    return pl.pallas_call(
        put_out,
        out_shape=tuple(jax.ShapeDtypeStruct(array.shape, array.dtype) for array in kept),
        in_specs=[inside] * 3,
        out_specs=(anywhere,) * 3,
        scratch_shapes=[dma((3,))],
        compiler_params=pltpu.CompilerParams(vmem_limit_bytes=2**20),
    )(*kept)


def solution(mesh):
    placed = (
        P("expert", "shard", None),
        P("expert", "shard", None),
        P("shard", "expert"),
        P("shard"),
    )
    return jax.shard_map(
        functools.partial(per_device, mesh.shape["shard"], mesh.shape["expert"]),
        mesh=mesh,
        in_specs=placed,
        out_specs=(P("expert", "shard", None), P("expert", "shard", None), P()),
        check_vma=False,
    )
```

profile of v0, /device:TPU:0, one launch (start us, length us, event | category | flops | bytes accessed | tf_op | source)
XLA Modules:
  0.0 560.6 jit_solution(4085885789385316818)
XLA Ops:
  0.6 551.0 %shard_map.67 = (bf16[32,96,2048]{2,1,0:T(8,128)(2,1)S(1)}, bf16[32,96,2048]{2,1,0:T(8,128)(2,1)S(1)}, bf16[2048,128]{1,0:T(8,128)(2,1)S(1)}) custom-call(f32[32,256,768]{2,1,0:T(8,128)} %gate.1, f32[32,256,768]{2,1,0:T(8,128)} %up.1, f32[32,256]{1,0:T(8,128)} %bitcast.2, f32[1,256]{1,0:T(1,128)} %bitcast.3), custom_call_target="tpu_custom_call" | custom-call | tf_op jit(solution)/shard_map/pallas_call | solution.py:208
  551.6 8.9 %shard_map.68 = (bf16[32,96,2048]{2,1,0:T(8,128)(2,1)}, bf16[32,96,2048]{2,1,0:T(8,128)(2,1)}, bf16[2048,128]{1,0:T(8,128)(2,1)}) custom-call(bf16[32,96,2048]{2,1,0:T(8,128)(2,1)S(1)} %get-tuple-element.6.gate, bf16[32,96,2048]{2,1,0:T(8,128)(2,1)S(1)} %get-tuple-element.7.up, bf16[2048,128]{1,0:T(8,128)(2,1)S(1)} %get-tuple-element.8.router), custom_call_target="tpu_custom_call" | custom-call | tf_op jit(solution)/shard_map/pallas_call | solution.py:224
where the time goes:
time: 561 us
  Pallas kernels  560 us (100%)
    pallas_call x1, Pallas kernels, per_device(): pl.pallas_call(functools.partial(kernel, shards, groups), out_shape=(fina...  551 us

commit v1 on v0

v1 whole, which is shorter than its diff:
```python
import functools

import jax
import jax.numpy as jnp
from jax import lax
from jax.experimental import pallas as pl
from jax.experimental.pallas import tpu as pltpu
from jax.sharding import PartitionSpec as P

NEAR = 1
PAIR = 2
CORES = 2
CHUNK = 1
WINDOW = 2
EVERY = 3
SLOTS = 4
LIMIT = 32
TAILS = (8, 2)
TAIL = max(TAILS)
PIECES = 4


def plain(master_gate, master_up, router_weight, router_gain):
    narrow_gate, narrow_up = (master_gate.astype(jnp.bfloat16), master_up.astype(jnp.bfloat16))
    final_gate, final_up = (
        lax.all_to_all(narrow_gate, "shard", split_axis=2, concat_axis=1, tiled=True),
        lax.all_to_all(narrow_up, "shard", split_axis=2, concat_axis=1, tiled=True),
    )
    final_gate = jnp.transpose(final_gate, (0, 2, 1))
    final_up = jnp.transpose(final_up, (0, 2, 1))
    part_router = (router_weight * router_gain[:, None]).astype(jnp.bfloat16)
    row_router = lax.all_gather(part_router, "shard", axis=0, tiled=True)
    serve_router = lax.all_gather(row_router, "expert", axis=1, tiled=True)
    return (final_gate, final_up, serve_router)


def columns(of, depth):
    return pl.ds(pl.multiple_of(of * depth, depth), depth)


def per_core(group, act):
    for core, tail in enumerate(TAILS):
        @pl.when(lax.rem(group, CORES) == core)
        def _():
            act(tail)


def to_peers(shards, me, least, most, act):
    place, side = me // PAIR, lax.rem(me, PAIR)
    for away in range(least, most + 1):
        for turned in range(0 if away else 1, PAIR):
            other = lax.rem(side + turned, PAIR)
            if away == 0:
                act(place * PAIR + other)
                continue

            @pl.when(place + away < shards // PAIR)
            def _():
                act((place + away) * PAIR + other)

            @pl.when(place >= away)
            def _():
                act((place - away) * PAIR + other)


def kernel(
    shards, groups, gate, up, weight, gain, out_gate, out_up, out_router, rest,
    held, coming, router, load_sem, own_sem, send_sem, recv_sem,
    row_send, row_recv, side_send, side_recv, column_send, column_recv, ready,
):
    me, group = lax.axis_index("shard"), lax.axis_index("expert")
    _, _, experts, rows, depth = held.shape
    width = weight.shape[0]
    places = shards // PAIR
    last = places - 1
    place, side = me // PAIR, lax.rem(me, PAIR)
    chunks, early = experts // CHUNK, experts - TAIL
    sources, outs = (gate, up), (out_gate, out_up)
    mine = columns(me, depth)
    my_part = pl.ds(pl.multiple_of(group * width, width), width)
    peers = functools.partial(to_peers, shards, me)
    above, below = place + 1 < places, place >= 1
    tail = TAILS[0]
    for core in range(1, CORES):
        tail = jnp.where(lax.rem(group, CORES) == core, TAILS[core], tail)
    total = 2 * chunks - tail // CHUNK

    barrier = pltpu.get_barrier_semaphore()
    peers(0, NEAR, lambda peer: pl.semaphore_signal(barrier, inc=1, device_id={"shard": peer}))
    for step in range(1, groups):
        pl.semaphore_signal(barrier, inc=1, device_id={"expert": lax.rem(group + step, groups)})

    def enter():
        sides = jnp.where(above, 1, 0) + jnp.where(below, 1, 0)
        pl.semaphore_wait(barrier, PAIR + groups - 2 + PAIR * sides)

    def tell(way, away):
        pl.semaphore_signal(
            ready.at[way, away], inc=1, device_id={"shard": me + (PAIR if way else -PAIR)}
        )

    def far_ready(away):
        @pl.when(place + away < places)
        def _():
            pl.semaphore_wait(ready.at[0, away], 1)

            @pl.when(below)
            def _():
                tell(0, away + 1)

        @pl.when(place >= away)
        def _():
            pl.semaphore_wait(ready.at[1, away], 1)

            @pl.when(above)
            def _():
                tell(1, away + 1)

    def load(which, expert):
        slot = lax.rem(expert, SLOTS)
        return pltpu.make_async_copy(sources[which].at[expert], coming.at[slot], load_sem.at[slot])

    def own(which, first, count):
        span = pl.ds(first, count)
        return pltpu.make_async_copy(
            held.at[which, me, span], outs[which].at[span, :, mine], own_sem
        )

    def send(which, peer, chunk):
        span = pl.ds(chunk * CHUNK, CHUNK)
        return pltpu.make_async_remote_copy(
            src_ref=held.at[which, peer, span],
            dst_ref=outs[which].at[span, :, mine],
            send_sem=send_sem.at[which * chunks + chunk],
            recv_sem=recv_sem.at[which * chunks + chunk],
            device_id={"shard": peer},
        )

    def settle(at):
        part = held.at[0, pl.ds(0, shards - 1), pl.ds(0, CHUNK)]
        pltpu.make_async_remote_copy(
            src_ref=part,
            dst_ref=part,
            send_sem=send_sem.at[at],
            recv_sem=recv_sem.at[at],
            device_id={"shard": lax.rem(me + 1, shards)},
        ).wait()

    def row(of, way):
        at = side * places + of
        return pltpu.make_async_remote_copy(
            src_ref=router.at[at, my_part],
            dst_ref=router.at[at, my_part],
            send_sem=row_send.at[of, way],
            recv_sem=row_recv.at[of],
            device_id={"shard": me + (PAIR if way else -PAIR)},
        )

    def pass_rows(away, act):
        @pl.when(above & (place >= away))
        def _():
            act(row(place - away, 1))

        @pl.when(below & (place + away < places))
        def _():
            act(row(place + away, 0))

    def rows_in(away):
        @pl.when(place >= away)
        def _():
            row(place - away, 1).wait_recv()

        @pl.when(place + away < places)
        def _():
            row(place + away, 0).wait_recv()

    def across(turned, of):
        part = router.at[pl.ds(of * places, places), my_part]
        other = lax.rem(side + turned, PAIR)
        return pltpu.make_async_remote_copy(
            src_ref=part,
            dst_ref=part,
            send_sem=side_send.at[other],
            recv_sem=side_recv.at[of],
            device_id={"shard": place * PAIR + other},
        )

    def column(peer, of):
        part = pl.ds(pl.multiple_of(of * width, width), width)
        return pltpu.make_async_remote_copy(
            src_ref=router.at[:, part],
            dst_ref=router.at[:, part],
            send_sem=column_send.at[peer],
            recv_sem=column_recv.at[of],
            device_id={"expert": peer},
        )

    def turn(which, expert):
        load(which, expert).wait()
        block = coming[lax.rem(expert, SLOTS)].T.astype(jnp.bfloat16)
        for peer in range(shards):
            held[which, peer, expert] = block[peer * rows:(peer + 1) * rows]
        if which == 1:
            @pl.when(expert >= early)
            def _():
                for peer in range(shards):
                    rest[peer, expert - early] = held[which, peer, expert]

        @pl.when(expert + SLOTS < experts)
        def _():
            load(which, expert + SLOTS).start()

    def turns(which, chunk):
        @pl.loop(0, CHUNK)
        def _(step):
            turn(which, chunk * CHUNK + step)

    def go(which, chunk):
        at = which * chunks + chunk
        if which == 1:
            settle(at - WINDOW)
        else:
            pl.when(at >= WINDOW)(lambda: settle(at - WINDOW))
        peers(NEAR, last, lambda peer: send(which, peer, chunk).start())
        peers(0, 0, lambda peer: send(which, peer, chunk).start())
        own(which, chunk * CHUNK, CHUNK).start()

    def pass_on(away):
        rows_in(away)
        pass_rows(away, lambda copy: copy.start())

    def pass_across():
        rows_in(last)
        for turned in range(1, PAIR):
            across(turned, side).start()

    def pass_columns():
        for turned in range(1, PAIR):
            across(turned, lax.rem(side + turned, PAIR)).wait_recv()
        for step in range(1, groups):
            column(lax.rem(group + step, groups), group).start()

    def write_router():
        for step in range(1, groups):
            peer = lax.rem(group + step, groups)
            column(peer, peer).wait_recv()
        for shard in range(shards):
            at = shard % PAIR * places + shard // PAIR
            out_router[shard * depth:(shard + 1) * depth] = router[at].T
        for away in range(last):
            pass_rows(away, lambda copy: copy.wait_send())
        for turned in range(1, PAIR):
            across(turned, side).wait_send()
        for step in range(1, groups):
            column(lax.rem(group + step, groups), group).wait_send()

    steps = [functools.partial(pass_on, away) for away in range(1, last)]
    steps += [pass_across, pass_columns, write_router]

    for first in range(SLOTS):
        load(0, first).start()
    router[side * places + place, my_part] = (weight[...] * gain[...]).astype(jnp.bfloat16)
    turns(0, 0)
    enter()

    @pl.when(above & below)
    def _():
        tell(0, 2)
        tell(1, 2)
    turns(0, 1)
    for away in range(NEAR, last + 1):
        if away > NEAR:
            far_ready(away)
        peers(away, away, lambda peer: send(0, peer, 0).start())
    peers(0, 0, lambda peer: send(0, peer, 0).start())
    own(0, 0, CHUNK).start()
    pass_rows(0, lambda copy: copy.start())

    @pl.loop(1, chunks - 1)
    def _(chunk):
        turns(0, chunk + 1)
        go(0, chunk)
        for at, act in enumerate(steps):
            pl.when(chunk == (at + 1) * EVERY)(act)
    for first in range(SLOTS):
        load(1, first).start()
    turns(1, 0)
    go(0, chunks - 1)

    @pl.loop(0, chunks)
    def _(chunk):
        pl.when(chunk + 1 < chunks)(lambda: turns(1, chunk + 1))
        pl.when(chunks + chunk < total)(lambda: go(1, chunk))

    @pl.loop(total - WINDOW, total)
    def _(at):
        settle(at)

    def finish(tail):
        own(0, 0, experts).wait()
        own(1, 0, experts - tail).wait()
    per_core(group, finish)


def second(shards, rest, token, out, own_sem, send_sem, recv_sem):
    del token
    me, group = lax.axis_index("shard"), lax.axis_index("expert")
    depth = rest.shape[3]
    last = shards // PAIR - 1
    peers = functools.partial(to_peers, shards, me)
    barrier = pltpu.get_barrier_semaphore()
    peers(0, last, lambda peer: pl.semaphore_signal(barrier, inc=1, device_id={"shard": peer}))
    pl.semaphore_wait(barrier, shards - 1)

    def send(peer, at):
        return pltpu.make_async_remote_copy(
            src_ref=rest.at[peer, at],
            dst_ref=out.at[at, :, columns(me, depth)],
            send_sem=send_sem.at[at],
            recv_sem=recv_sem.at[at],
            device_id={"shard": peer},
        )

    def settle(at):
        part = rest.at[pl.ds(0, shards - 1), 0]
        pltpu.make_async_remote_copy(
            src_ref=part,
            dst_ref=part,
            send_sem=send_sem.at[at],
            recv_sem=recv_sem.at[at],
            device_id={"shard": lax.rem(me + 1, shards)},
        ).wait()

    def exchange(tail):
        span = pl.ds(TAIL - tail, tail)
        for at in range(TAIL - tail, TAIL):
            if at - WINDOW >= TAIL - tail:
                settle(at - WINDOW)
            peers(1, last, lambda peer: send(peer, at).start())
            peers(0, 0, lambda peer: send(peer, at).start())
        own = pltpu.make_async_copy(rest.at[me, span], out.at[span, :, columns(me, depth)], own_sem)
        own.start()
        own.wait()
        for at in range(max(TAIL - WINDOW, TAIL - tail), TAIL):
            settle(at)
    per_core(group, exchange)


def put_out(gate, up, router, out_gate, out_up, out_router, token, sem):
    experts, early = gate.shape[0], gate.shape[0] - TAIL
    token[...] = jnp.zeros_like(token)

    def copy(source, out, first, count, at):
        span = pl.ds(first, count)
        return pltpu.make_async_copy(source.at[span], out.at[span], sem.at[at])

    copies = [pltpu.make_async_copy(router, out_router, sem.at[0])]
    for source, out, count in ((gate, out_gate, experts), (up, out_up, early)):
        for piece in range(PIECES):
            first = count * piece // PIECES
            copies.append(copy(source, out, first, count * (piece + 1) // PIECES - first, len(copies)))
    for one in copies:
        one.start()

    def more(tail):
        if tail < TAIL:
            one = copy(up, out_up, early, TAIL - tail, len(copies))
            one.start()
            one.wait()
    per_core(lax.axis_index("expert"), more)
    for one in copies:
        one.wait()


def put_rest(rest, already, out, sem):
    del already

    def put(tail):
        first = out.shape[0] - tail
        copies = [
            pltpu.make_async_copy(rest.at[TAIL - tail + at], out.at[first + at], sem.at[at])
            for at in range(tail)
        ]
        for one in copies:
            one.start()
        for one in copies:
            one.wait()
    per_core(lax.axis_index("expert"), put)


def per_device(shards, groups, master_gate, master_up, router_weight, router_gain):
    experts, depth, inner = master_gate.shape
    width = router_weight.shape[1]
    rows = inner // shards
    places = shards // PAIR
    if (
        shards % PAIR or depth % 128 or rows % 16 or width % 16 or experts % CHUNK or experts < 3 * TAIL
        or (width * groups) % 128 or groups % CORES
        or places < 2 or experts // CHUNK < (places + 2) * EVERY
    ):
        return plain(master_gate, master_up, router_weight, router_gain)
    anywhere = pl.BlockSpec(memory_space=pl.ANY)
    inside = pl.BlockSpec(memory_space=pltpu.VMEM)
    final = (experts, rows, shards * depth)
    dma = pltpu.SemaphoreType.DMA
    gate, up, router, rest = pl.pallas_call(
        functools.partial(kernel, shards, groups),
        out_shape=(
            pltpu.VMEM(final, jnp.bfloat16),
            pltpu.VMEM((experts - min(TAILS), *final[1:]), jnp.bfloat16),
            pltpu.VMEM((shards * depth, groups * width), jnp.bfloat16),
            pltpu.VMEM((shards, TAIL, rows, depth), jnp.bfloat16),
        ),
        in_specs=[anywhere, anywhere, inside, inside],
        out_specs=(inside,) * 4,
        scratch_shapes=[
            pltpu.VMEM((2, shards, experts, rows, depth), jnp.bfloat16),
            pltpu.VMEM((SLOTS, depth, inner), jnp.float32),
            pltpu.VMEM((shards, groups * width, depth), jnp.bfloat16),
            dma((SLOTS,)), dma, dma((2 * experts // CHUNK,)), dma((2 * experts // CHUNK,)),
            dma((places, 2)), dma((places,)), dma((PAIR,)), dma((PAIR,)), dma((groups,)), dma((groups,)),
            pltpu.SemaphoreType.REGULAR((2, places + 1)),
        ],
        compiler_params=pltpu.CompilerParams(
            collective_id=0, has_side_effects=True, vmem_limit_bytes=LIMIT * 2**20
        ),
    )(master_gate, master_up, router_weight.T, router_gain[None])
    out = jax.ShapeDtypeStruct(final, jnp.bfloat16)
    final_gate, most_up, serve_router, token = pl.pallas_call(
        put_out,
        out_shape=(
            out, out, jax.ShapeDtypeStruct(router.shape, router.dtype), pltpu.VMEM((8, 128), jnp.float32)
        ),
        in_specs=[inside] * 3,
        out_specs=(anywhere,) * 3 + (inside,),
        scratch_shapes=[dma((2 * PIECES + 2,))],
        compiler_params=pltpu.CompilerParams(vmem_limit_bytes=2**20),
    )(gate, up, router)
    last_up = pl.pallas_call(
        functools.partial(second, shards),
        out_shape=pltpu.VMEM((TAIL, *final[1:]), jnp.bfloat16),
        in_specs=[inside] * 2,
        out_specs=inside,
        scratch_shapes=[dma, dma((TAIL,)), dma((TAIL,))],
        compiler_params=pltpu.CompilerParams(
            collective_id=1, has_side_effects=True, vmem_limit_bytes=2**20
        ),
    )(rest, token)
    final_up = pl.pallas_call(
        put_rest,
        out_shape=out,
        in_specs=[inside, anywhere],
        out_specs=anywhere,
        input_output_aliases={1: 0},
        scratch_shapes=[dma((TAIL,))],
        compiler_params=pltpu.CompilerParams(vmem_limit_bytes=2**20),
    )(last_up, most_up)
    return final_gate, final_up, serve_router


def solution(mesh):
    placed = (
        P("expert", "shard", None),
        P("expert", "shard", None),
        P("shard", "expert"),
        P("shard"),
    )
    return jax.shard_map(
        functools.partial(per_device, mesh.shape["shard"], mesh.shape["expert"]),
        mesh=mesh,
        in_specs=placed,
        out_specs=(P("expert", "shard", None), P("expert", "shard", None), P()),
        check_vma=False,
    )
```

time: 561 us -> 552 us (0.984)
  Pallas kernels: 560 us -> 551 us
    pallas_call x2 -> x4, Pallas kernels: 560 us -> 551 us  [the longest x1 486 us: per_device(): pl.pallas_call(functools.partial(kernel, shards, groups), out_shape=(pltp...]
where the time goes in v1:
time: 552 us
  Pallas kernels  551 us (100%)
    pallas_call x1, Pallas kernels, per_device(): pl.pallas_call(functools.partial(kernel, shards, groups), out_shape=(pltp...  486 us
    pallas_call x1, Pallas kernels, per_device(): pl.pallas_call(functools.partial(second, shards), out_shape=pltpu.VMEM((T...  55.6 us

profile of v1, /device:TPU:0, one launch (start us, length us, event | category | flops | bytes accessed | tf_op | source)
XLA Modules:
  0.0 551.8 jit_solution(7383709740078588429)
XLA Ops:
  0.6 486.1 %shard_map.67 = (bf16[32,96,2048]{2,1,0:T(8,128)(2,1)S(1)}, bf16[30,96,2048]{2,1,0:T(8,128)(2,1)S(1)}, bf16[2048,128]{1,0:T(8,128)(2,1)S(1)}, bf16[8,8,96,256]{3,2,1,0:T(8,128)(2,1)S(1)}) custom-call(f32[32,256,768]{2,1,0:T(8,128)} %gate.1, f32[32,256,768]{2,1,0:T(8,128)} %up.1, f32[32,256]{1,0:T(8,128)} %bitcast.2, f32[1,256]{1,0:T(1,128)} %bitcast.3), custom_call_target="tpu_custom_call" | custom-call | tf_op jit(solution)/shard_map/pallas_call | solution.py:406
  486.7 7.8 %shard_map.68 = (bf16[32,96,2048]{2,1,0:T(8,128)(2,1)}, bf16[32,96,2048]{2,1,0:T(8,128)(2,1)}, bf16[2048,128]{1,0:T(8,128)(2,1)}, f32[8,128]{1,0:T(8,128)S(1)}) custom-call(bf16[32,96,2048]{2,1,0:T(8,128)(2,1)S(1)} %get-tuple-element.11.gate, bf16[30,96,2048]{2,1,0:T(8,128)(2,1)S(1)} %get-tuple-element.12.up, bf16[2048,128]{1,0:T(8,128)(2,1)S(1)} %get-tuple-element.13.router), custom_call_target="tpu_custom_call" | custom-call | tf_op jit(solution)/shard_map/pallas_call | solution.py:429
  494.5 55.6 %shard_map.69.rest = bf16[8,96,2048]{2,1,0:T(8,128)(2,1)S(1)} custom-call(bf16[8,8,96,256]{3,2,1,0:T(8,128)(2,1)S(1)} %get-tuple-element.15.rest, f32[8,128]{1,0:T(8,128)S(1)} %get-tuple-element.16.token), custom_call_target="tpu_custom_call" | custom-call | tf_op jit(solution)/shard_map/pallas_call | solution.py:439
  550.1 1.7 shard_map.70

commit v2 on v1

--- a/solution.py
+++ b/solution.py
@@ -10,12 +10,13 @@
 NEAR = 1
 PAIR = 2
 CORES = 2
-CHUNK = 1
 WINDOW = 2
+LATER = 4
+LEAD = 6
 EVERY = 3
 SLOTS = 4
 LIMIT = 32
-TAILS = (8, 2)
+TAILS = (7, 2)
 TAIL = max(TAILS)
 PIECES = 4
 
@@ -64,18 +65,18 @@
 
 
 def kernel(
-    shards, groups, gate, up, weight, gain, out_gate, out_up, out_router, rest,
+    shards, groups, gate, up, weight, gain, out, out_router, rest,
     held, coming, router, load_sem, own_sem, send_sem, recv_sem,
     row_send, row_recv, side_send, side_recv, column_send, column_recv, ready,
 ):
     me, group = lax.axis_index("shard"), lax.axis_index("expert")
-    _, _, experts, rows, depth = held.shape
+    _, units, rows, depth = held.shape
+    experts = units // 2
     width = weight.shape[0]
     places = shards // PAIR
     last = places - 1
     place, side = me // PAIR, lax.rem(me, PAIR)
-    chunks, early = experts // CHUNK, experts - TAIL
-    sources, outs = (gate, up), (out_gate, out_up)
+    early = units - TAIL
     mine = columns(me, depth)
     my_part = pl.ds(pl.multiple_of(group * width, width), width)
     peers = functools.partial(to_peers, shards, me)
@@ -83,7 +84,7 @@
     tail = TAILS[0]
     for core in range(1, CORES):
         tail = jnp.where(lax.rem(group, CORES) == core, TAILS[core], tail)
-    total = 2 * chunks - tail // CHUNK
+    total = units - tail
 
     barrier = pltpu.get_barrier_semaphore()
     peers(0, NEAR, lambda peer: pl.semaphore_signal(barrier, inc=1, device_id={"shard": peer}))
@@ -116,28 +117,30 @@
             def _():
                 tell(1, away + 1)
 
-    def load(which, expert):
-        slot = lax.rem(expert, SLOTS)
-        return pltpu.make_async_copy(sources[which].at[expert], coming.at[slot], load_sem.at[slot])
-
-    def own(which, first, count):
+    def load(at, act):
+        slot = lax.rem(at, SLOTS)
+        for which, source in enumerate((gate, up)):
+            @pl.when(at < experts if which == 0 else (at >= experts) & (at < units))
+            def _():
+                act(pltpu.make_async_copy(
+                    source.at[at - which * experts], coming.at[slot], load_sem.at[slot]
+                ))
+
+    def own(first, count):
         span = pl.ds(first, count)
-        return pltpu.make_async_copy(
-            held.at[which, me, span], outs[which].at[span, :, mine], own_sem
-        )
-
-    def send(which, peer, chunk):
-        span = pl.ds(chunk * CHUNK, CHUNK)
+        return pltpu.make_async_copy(held.at[me, span], out.at[span, :, mine], own_sem)
+
+    def send(peer, at):
         return pltpu.make_async_remote_copy(
-            src_ref=held.at[which, peer, span],
-            dst_ref=outs[which].at[span, :, mine],
-            send_sem=send_sem.at[which * chunks + chunk],
-            recv_sem=recv_sem.at[which * chunks + chunk],
+            src_ref=held.at[peer, at],
+            dst_ref=out.at[at, :, mine],
+            send_sem=send_sem.at[at],
+            recv_sem=recv_sem.at[at],
             device_id={"shard": peer},
         )
 
     def settle(at):
-        part = held.at[0, pl.ds(0, shards - 1), pl.ds(0, CHUNK)]
+        part = held.at[0, pl.ds(0, shards - 1)]
         pltpu.make_async_remote_copy(
             src_ref=part,
             dst_ref=part,
@@ -195,35 +198,27 @@
             device_id={"expert": peer},
         )
 
-    def turn(which, expert):
-        load(which, expert).wait()
-        block = coming[lax.rem(expert, SLOTS)].T.astype(jnp.bfloat16)
+    def turn(at, more=(SLOTS,)):
+        load(at, lambda copy: copy.wait())
+        for ahead in more[:-1]:
+            load(at + ahead, lambda copy: copy.start())
+        block = coming[lax.rem(at, SLOTS)].T.astype(jnp.bfloat16)
         for peer in range(shards):
-            held[which, peer, expert] = block[peer * rows:(peer + 1) * rows]
-        if which == 1:
-            @pl.when(expert >= early)
-            def _():
-                for peer in range(shards):
-                    rest[peer, expert - early] = held[which, peer, expert]
-
-        @pl.when(expert + SLOTS < experts)
-        def _():
-            load(which, expert + SLOTS).start()
-
-    def turns(which, chunk):
-        @pl.loop(0, CHUNK)
-        def _(step):
-            turn(which, chunk * CHUNK + step)
-
-    def go(which, chunk):
-        at = which * chunks + chunk
-        if which == 1:
-            settle(at - WINDOW)
-        else:
-            pl.when(at >= WINDOW)(lambda: settle(at - WINDOW))
-        peers(NEAR, last, lambda peer: send(which, peer, chunk).start())
-        peers(0, 0, lambda peer: send(which, peer, chunk).start())
-        own(which, chunk * CHUNK, CHUNK).start()
+            held[peer, at] = block[peer * rows:(peer + 1) * rows]
+
+        @pl.when(at >= early)
+        def _():
+            for peer in range(shards):
+                rest[peer, at - early] = held[peer, at]
+        load(at + more[-1], lambda copy: copy.start())
+
+    def near(at):
+        peers(NEAR, NEAR, lambda peer: send(peer, at).start())
+        peers(0, 0, lambda peer: send(peer, at).start())
+        own(at, 1).start()
+
+    def far(at):
+        peers(NEAR + 1, last, lambda peer: send(peer, at).start())
 
     def pass_on(away):
         rows_in(away)
@@ -257,49 +252,41 @@
     steps = [functools.partial(pass_on, away) for away in range(1, last)]
     steps += [pass_across, pass_columns, write_router]
 
-    for first in range(SLOTS):
-        load(0, first).start()
+    load(0, lambda copy: copy.start())
     router[side * places + place, my_part] = (weight[...] * gain[...]).astype(jnp.bfloat16)
-    turns(0, 0)
+    turn(0, range(1, SLOTS + 1))
     enter()
 
     @pl.when(above & below)
     def _():
         tell(0, 2)
         tell(1, 2)
-    turns(0, 1)
-    for away in range(NEAR, last + 1):
-        if away > NEAR:
-            far_ready(away)
-        peers(away, away, lambda peer: send(0, peer, 0).start())
-    peers(0, 0, lambda peer: send(0, peer, 0).start())
-    own(0, 0, CHUNK).start()
+    near(0)
     pass_rows(0, lambda copy: copy.start())
 
-    @pl.loop(1, chunks - 1)
-    def _(chunk):
-        turns(0, chunk + 1)
-        go(0, chunk)
-        for at, act in enumerate(steps):
-            pl.when(chunk == (at + 1) * EVERY)(act)
-    for first in range(SLOTS):
-        load(1, first).start()
-    turns(1, 0)
-    go(0, chunks - 1)
-
-    @pl.loop(0, chunks)
-    def _(chunk):
-        pl.when(chunk + 1 < chunks)(lambda: turns(1, chunk + 1))
-        pl.when(chunks + chunk < total)(lambda: go(1, chunk))
+    @pl.loop(1, LEAD + 1)
+    def _(at):
+        turn(at)
+        pl.when(at < LEAD)(lambda: near(at))
+    for away in range(NEAR + 1, last + 1):
+        far_ready(away)
+
+    @pl.loop(0, units)
+    def _(at):
+        pl.when(at + LEAD + 1 < units)(lambda: turn(at + LEAD + 1))
+
+        @pl.when(at < total)
+        def _():
+            pl.when(at >= WINDOW)(lambda: settle(at - WINDOW))
+            pl.when(at + LEAD < total)(lambda: near(at + LEAD))
+            far(at)
+        for step, act in enumerate(steps):
+            pl.when(at == (step + 1) * EVERY)(act)
 
     @pl.loop(total - WINDOW, total)
     def _(at):
         settle(at)
-
-    def finish(tail):
-        own(0, 0, experts).wait()
-        own(1, 0, experts - tail).wait()
-    per_core(group, finish)
+    per_core(group, lambda tail: own(0, units - tail).wait())
 
 
 def second(shards, rest, token, out, own_sem, send_sem, recv_sem):
@@ -334,37 +321,41 @@
     def exchange(tail):
         span = pl.ds(TAIL - tail, tail)
         for at in range(TAIL - tail, TAIL):
-            if at - WINDOW >= TAIL - tail:
-                settle(at - WINDOW)
+            if at - LATER >= TAIL - tail:
+                settle(at - LATER)
             peers(1, last, lambda peer: send(peer, at).start())
             peers(0, 0, lambda peer: send(peer, at).start())
         own = pltpu.make_async_copy(rest.at[me, span], out.at[span, :, columns(me, depth)], own_sem)
         own.start()
         own.wait()
-        for at in range(max(TAIL - WINDOW, TAIL - tail), TAIL):
+        for at in range(max(TAIL - LATER, TAIL - tail), TAIL):
             settle(at)
     per_core(group, exchange)
 
 
-def put_out(gate, up, router, out_gate, out_up, out_router, token, sem):
-    experts, early = gate.shape[0], gate.shape[0] - TAIL
+def put_out(kept, router, out_gate, out_up, out_router, token, sem):
+    experts = out_gate.shape[0]
+    early = experts - TAIL
     token[...] = jnp.zeros_like(token)
 
-    def copy(source, out, first, count, at):
-        span = pl.ds(first, count)
-        return pltpu.make_async_copy(source.at[span], out.at[span], sem.at[at])
+    def copy(which, first, count, at):
+        return pltpu.make_async_copy(
+            kept.at[pl.ds(which * experts + first, count)],
+            (out_gate, out_up)[which].at[pl.ds(first, count)],
+            sem.at[at],
+        )
 
     copies = [pltpu.make_async_copy(router, out_router, sem.at[0])]
-    for source, out, count in ((gate, out_gate, experts), (up, out_up, early)):
+    for which, count in enumerate((experts, early)):
         for piece in range(PIECES):
             first = count * piece // PIECES
-            copies.append(copy(source, out, first, count * (piece + 1) // PIECES - first, len(copies)))
+            copies.append(copy(which, first, count * (piece + 1) // PIECES - first, len(copies)))
     for one in copies:
         one.start()
 
     def more(tail):
         if tail < TAIL:
-            one = copy(up, out_up, early, TAIL - tail, len(copies))
+            one = copy(1, early, TAIL - tail, len(copies))
             one.start()
             one.wait()
     per_core(lax.axis_index("expert"), more)
@@ -394,30 +385,29 @@
     rows = inner // shards
     places = shards // PAIR
     if (
-        shards % PAIR or depth % 128 or rows % 16 or width % 16 or experts % CHUNK or experts < 3 * TAIL
+        shards % PAIR or depth % 128 or rows % 16 or width % 16 or experts < 3 * TAIL
         or (width * groups) % 128 or groups % CORES
-        or places < 2 or experts // CHUNK < (places + 2) * EVERY
+        or places < 2 or experts < (places + 2) * EVERY
     ):
         return plain(master_gate, master_up, router_weight, router_gain)
     anywhere = pl.BlockSpec(memory_space=pl.ANY)
     inside = pl.BlockSpec(memory_space=pltpu.VMEM)
     final = (experts, rows, shards * depth)
     dma = pltpu.SemaphoreType.DMA
-    gate, up, router, rest = pl.pallas_call(
+    kept, router, rest = pl.pallas_call(
         functools.partial(kernel, shards, groups),
         out_shape=(
-            pltpu.VMEM(final, jnp.bfloat16),
-            pltpu.VMEM((experts - min(TAILS), *final[1:]), jnp.bfloat16),
+            pltpu.VMEM((2 * experts - min(TAILS), *final[1:]), jnp.bfloat16),
             pltpu.VMEM((shards * depth, groups * width), jnp.bfloat16),
             pltpu.VMEM((shards, TAIL, rows, depth), jnp.bfloat16),
         ),
         in_specs=[anywhere, anywhere, inside, inside],
-        out_specs=(inside,) * 4,
+        out_specs=(inside,) * 3,
         scratch_shapes=[
-            pltpu.VMEM((2, shards, experts, rows, depth), jnp.bfloat16),
+            pltpu.VMEM((shards, 2 * experts, rows, depth), jnp.bfloat16),
             pltpu.VMEM((SLOTS, depth, inner), jnp.float32),
             pltpu.VMEM((shards, groups * width, depth), jnp.bfloat16),
-            dma((SLOTS,)), dma, dma((2 * experts // CHUNK,)), dma((2 * experts // CHUNK,)),
+            dma((SLOTS,)), dma, dma((2 * experts,)), dma((2 * experts,)),
             dma((places, 2)), dma((places,)), dma((PAIR,)), dma((PAIR,)), dma((groups,)), dma((groups,)),
             pltpu.SemaphoreType.REGULAR((2, places + 1)),
         ],
@@ -431,12 +421,12 @@
         out_shape=(
             out, out, jax.ShapeDtypeStruct(router.shape, router.dtype), pltpu.VMEM((8, 128), jnp.float32)
         ),
-        in_specs=[inside] * 3,
+        in_specs=[inside] * 2,
         out_specs=(anywhere,) * 3 + (inside,),
         scratch_shapes=[dma((2 * PIECES + 2,))],
         compiler_params=pltpu.CompilerParams(vmem_limit_bytes=2**20),
-    )(gate, up, router)
-    last_up = pl.pallas_call(
+    )(kept, router)
+    kept_rest = pl.pallas_call(
         functools.partial(second, shards),
         out_shape=pltpu.VMEM((TAIL, *final[1:]), jnp.bfloat16),
         in_specs=[inside] * 2,
@@ -454,7 +444,7 @@
         input_output_aliases={1: 0},
         scratch_shapes=[dma((TAIL,))],
         compiler_params=pltpu.CompilerParams(vmem_limit_bytes=2**20),
-    )(last_up, most_up)
+    )(kept_rest, most_up)
     return final_gate, final_up, serve_router
 
 

time: 552 us -> 551 us (level)
    pallas_call x1, Pallas kernels: 55.6 us -> 49.2 us  [per_device(): pl.pallas_call(functools.partial(second, shards), out_shape=pltpu.VMEM((T...]
where the time goes in v2:
time: 551 us; the launch traced here: 549 us
  Pallas kernels  549 us (100%)
    pallas_call x1, Pallas kernels, per_device(): pl.pallas_call(functools.partial(kernel, shards, groups), out_shape=(pltp...  490 us
    pallas_call x1, Pallas kernels, per_device(): pl.pallas_call(functools.partial(second, shards), out_shape=pltpu.VMEM((T...  49.2 us

profile of v2, /device:TPU:0, one launch (start us, length us, event | category | flops | bytes accessed | tf_op | source)
XLA Modules:
  0.0 549.5 jit_solution(5335755509983857532)
XLA Ops:
  0.6 490.1 %shard_map.67 = (bf16[62,96,2048]{2,1,0:T(8,128)(2,1)S(1)}, bf16[2048,128]{1,0:T(8,128)(2,1)S(1)}, bf16[8,7,96,256]{3,2,1,0:T(8,128)(2,1)S(1)}) custom-call(f32[32,256,768]{2,1,0:T(8,128)} %gate.1, f32[32,256,768]{2,1,0:T(8,128)} %up.1, f32[32,256]{1,0:T(8,128)} %bitcast.2, f32[1,256]{1,0:T(1,128)} %bitcast.3), custom_call_target="tpu_custom_call" | custom-call | tf_op jit(solution)/shard_map/pallas_call | solution.py:397
  490.8 7.9 %shard_map.68 = (bf16[32,96,2048]{2,1,0:T(8,128)(2,1)}, bf16[32,96,2048]{2,1,0:T(8,128)(2,1)}, bf16[2048,128]{1,0:T(8,128)(2,1)}, f32[8,128]{1,0:T(8,128)S(1)}) custom-call(bf16[62,96,2048]{2,1,0:T(8,128)(2,1)S(1)} %get-tuple-element.10.kept, bf16[2048,128]{1,0:T(8,128)(2,1)S(1)} %get-tuple-element.11.router), custom_call_target="tpu_custom_call" | custom-call | tf_op jit(solution)/shard_map/pallas_call | solution.py:419
  498.6 49.2 %shard_map.69.rest = bf16[7,96,2048]{2,1,0:T(8,128)(2,1)S(1)} custom-call(bf16[8,7,96,256]{3,2,1,0:T(8,128)(2,1)S(1)} %get-tuple-element.13.rest, f32[8,128]{1,0:T(8,128)S(1)} %get-tuple-element.14.token), custom_call_target="tpu_custom_call" | custom-call | tf_op jit(solution)/shard_map/pallas_call | solution.py:429
  547.9 1.6 shard_map.70

commit v3 on v2

--- a/solution.py
+++ b/solution.py
@@ -12,11 +12,11 @@
 CORES = 2
 WINDOW = 2
 LATER = 4
-LEAD = 6
+LEAD = 16
 EVERY = 3
 SLOTS = 4
 LIMIT = 32
-TAILS = (7, 2)
+TAILS = (6, 2)
 TAIL = max(TAILS)
 PIECES = 4
 

time: 551 us -> 552 us (level); the launches traced: 549 us -> 545 us
    pallas_call x1, Pallas kernels: 49.2 us -> 38.3 us  [per_device(): pl.pallas_call(functools.partial(second, shards), out_shape=pltpu.VMEM((T...]
    pallas_call x1, Pallas kernels: 490 us -> 496 us  [per_device(): pl.pallas_call(functools.partial(kernel, shards, groups), out_shape=(pltp...]
where the time goes in v3:
time: 552 us; the launch traced here: 545 us
  Pallas kernels  544 us (99%)
    pallas_call x1, Pallas kernels, per_device(): pl.pallas_call(functools.partial(kernel, shards, groups), out_shape=(pltp...  496 us
    pallas_call x1, Pallas kernels, per_device(): pl.pallas_call(functools.partial(second, shards), out_shape=pltpu.VMEM((T...  38.3 us

profile of v3, /device:TPU:0, one launch (start us, length us, event | category | flops | bytes accessed | tf_op | source)
XLA Modules:
  0.0 544.7 jit_solution(4722845604876914378)
XLA Ops:
  0.6 496.3 %shard_map.67 = (bf16[62,96,2048]{2,1,0:T(8,128)(2,1)S(1)}, bf16[2048,128]{1,0:T(8,128)(2,1)S(1)}, bf16[8,6,96,256]{3,2,1,0:T(8,128)(2,1)S(1)}) custom-call(f32[32,256,768]{2,1,0:T(8,128)} %gate.1, f32[32,256,768]{2,1,0:T(8,128)} %up.1, f32[32,256]{1,0:T(8,128)} %bitcast.2, f32[1,256]{1,0:T(1,128)} %bitcast.3), custom_call_target="tpu_custom_call" | custom-call | tf_op jit(solution)/shard_map/pallas_call | solution.py:397
  496.9 8.0 %shard_map.68 = (bf16[32,96,2048]{2,1,0:T(8,128)(2,1)}, bf16[32,96,2048]{2,1,0:T(8,128)(2,1)}, bf16[2048,128]{1,0:T(8,128)(2,1)}, f32[8,128]{1,0:T(8,128)S(1)}) custom-call(bf16[62,96,2048]{2,1,0:T(8,128)(2,1)S(1)} %get-tuple-element.10.kept, bf16[2048,128]{1,0:T(8,128)(2,1)S(1)} %get-tuple-element.11.router), custom_call_target="tpu_custom_call" | custom-call | tf_op jit(solution)/shard_map/pallas_call | solution.py:419
  504.9 38.3 %shard_map.69.rest = bf16[6,96,2048]{2,1,0:T(8,128)(2,1)S(1)} custom-call(bf16[8,6,96,256]{3,2,1,0:T(8,128)(2,1)S(1)} %get-tuple-element.13.rest, f32[8,128]{1,0:T(8,128)S(1)} %get-tuple-element.14.token), custom_call_target="tpu_custom_call" | custom-call | tf_op jit(solution)/shard_map/pallas_call | solution.py:429
  543.2 1.5 shard_map.70
